TPU v7x, 256 devices: a whole 4x4x8 slice. The times are simulated.
256 devices in a mesh: gx: 16 (over z_lo, x), gy: 4 (over y), gz: 4 (over z_hi, core).
Axes of the slice: x: 4, y: 4, z: 8 (z_hi: 2, z_lo: 4; z = z_hi * 4 + z_lo), core: 2. Of those that a mesh axis runs over, the one named last changes fastest.
Arguments:
- tokens: bfloat16 [8192, 4608], P('gx', 'gy'), may hold values from -6 to 6
- base_up_weight: bfloat16 [4608, 18432], P('gy', ('gz', 'gx')), may hold values from -0.09375 to 0.09375
- adapter_down_weight: bfloat16 [64, 16, 4608], P(None, None, 'gy'), may hold values from -0.09375 to 0.09375
- adapter_up_weight: bfloat16 [64, 16, 18432], P('gx', None, 'gz'), may hold values from -1.5 to 1.5
- block_adapter_index: int32 [64], P('gx'), may hold values from 0 to 63
- request_rows: int32 [64], P('gx'), may hold values from 1 to 128
Outputs:
- projected: bfloat16 [8192, 18432], P(('gx', 'gy'), 'gz')
Inputs may be any that keep to these rules, and one draw needn't show every extreme that they name: `request_rows`: live rows of each block.
All inputs are finite; a program needn't handle non-finite values.
Results may differ from a plain program's by a relative error of at most 0.0047.
Values may be sent and summed in bfloat16 or wider, within the bound.
A program may use at most 128 MiB of HBM per device.

v0:
```python
import jax
import jax.numpy as jnp
from jax import lax
from jax.sharding import PartitionSpec as P

ADAPTER_COUNT = 64
BLOCK = 128


def sent_to_all(array, axis):
    size = lax.axis_size(axis)
    return lax.all_to_all(
        jnp.broadcast_to(array[None], (size, *array.shape)), axis, 0, 0, tiled=True
    )


def taken_together(array, axis):
    return sent_to_all(array, axis).sum(axis=0)


def in_blocks(array, dim, size):
    before, after = (array.shape[:dim], array.shape[dim + 1 :])
    return jnp.moveaxis(array.reshape(*before, size, -1, *after), dim, 0)


def summed_on_arrival(array, axis, dim):
    size = lax.axis_size(axis)
    tiles = lax.all_to_all(in_blocks(array, dim, size), axis, 0, 0, tiled=True)
    return jnp.sum(tiles.astype(jnp.float32), axis=0)


def body(
    tokens,
    base_up_weight,
    adapter_down_weight,
    adapter_up_weight,
    block_adapter_index,
    request_rows,
):
    rows, shard_width = tokens.shape
    groups = lax.axis_size("gy")
    blocks = rows // BLOCK
    own_blocks = blocks // groups
    own_rows = own_blocks * BLOCK
    first = lax.axis_index("gy") * own_blocks
    rank_values = adapter_down_weight.shape[1]
    catalog = jnp.arange(ADAPTER_COUNT, dtype=jnp.int32)
    selected_adapters = (block_adapter_index[:, None] == catalog[None, :]).astype(jnp.bfloat16)
    chosen_down = jnp.dot(
        selected_adapters,
        adapter_down_weight.reshape(ADAPTER_COUNT, rank_values * shard_width),
        preferred_element_type=jnp.float32,
    )
    chosen_down = chosen_down.astype(jnp.bfloat16).reshape(blocks, rank_values, shard_width)
    tok_blocks = tokens.reshape(blocks, BLOCK, shard_width)
    shrink_part = jnp.einsum(
        "bmd,brd->bmr", tok_blocks, chosen_down, preferred_element_type=jnp.float32
    )
    shrink_all = taken_together(shrink_part, "gy")
    shrink_own = lax.dynamic_slice_in_dim(shrink_all, first, own_blocks, 0)
    shrink_low = shrink_own.astype(jnp.bfloat16)
    adapter_factors = lax.all_gather(adapter_up_weight, "gx", axis=0, tiled=True)
    out_width = adapter_factors.shape[2]
    own_picks = lax.dynamic_slice_in_dim(selected_adapters, first, own_blocks, 0)
    chosen_up = jnp.dot(
        own_picks,
        adapter_factors.reshape(ADAPTER_COUNT, rank_values * out_width),
        preferred_element_type=jnp.float32,
    )
    chosen_up = chosen_up.astype(jnp.bfloat16).reshape(own_blocks, rank_values, out_width)
    expand = jnp.einsum("bmr,brf->bmf", shrink_low, chosen_up, preferred_element_type=jnp.float32)
    expand = expand.reshape(own_rows, out_width)
    partial_value = jnp.dot(
        tokens,
        lax.all_gather(base_up_weight, "gx", axis=1, tiled=True),
        preferred_element_type=jnp.float32,
    )
    extra = 2.0 * expand
    total = summed_on_arrival(partial_value.astype(jnp.bfloat16), "gy", 0) + extra
    own_live = lax.dynamic_slice_in_dim(request_rows, first, own_blocks, 0)
    live_mask = (jnp.arange(BLOCK, dtype=jnp.int32)[None, :] < own_live[:, None]).reshape(
        own_rows, 1
    )
    return jnp.where(live_mask, total, 0.0).astype(jnp.bfloat16)


def solution(mesh):
    in_specs = (
        P("gx", "gy"),
        P("gy", ("gz", "gx")),
        P(None, None, "gy"),
        P("gx", None, "gz"),
        P("gx"),
        P("gx"),
    )
    out_specs = P(("gx", "gy"), "gz")
    return jax.shard_map(body, mesh=mesh, in_specs=in_specs, out_specs=out_specs, check_vma=False)
```

profile of v0, /device:TPU:1, one launch (start us, length us, event | category | flops | bytes accessed | tf_op | source)
XLA Modules:
  0.0 278.8 jit_solution(411881308684127946)
XLA Ops:
  6.5 0.0 copy-start
  6.5 0.0 all-gather.3.cloned.1.call-start
  6.5 0.7 all-gather.3.cloned.1.call-update
  7.3 0.0 all-gather.5.cloned.1.call-start
  7.3 0.7 all-gather.5.cloned.1.call-update
  8.0 2.2 copy.8
  10.2 0.5 convolution_convert_fusion
  10.7 0.4 convolution_bitcast_fusion
  11.2 0.7 broadcast_in_dim.11
  11.8 5.0 %all-to-all-start.1 = ((f32[4,4,128,16]{2,3,1,0:T(8,128)}), f32[4,4,128,16]{2,3,1,0:T(8,128)S(1)}, u32[]{:S(2)}, u32[]{:S(2)}) async-start(f32[4,4,128,16]{2,3,1,0:T(8,128)} %broadcast_in_dim.11), calls=%async_computation.1 | async-start | bytes 262144 | tf_op jit(solution)/shard_map/all_to_all | solution.py:12
  16.9 120.7 %all-gather.3.cloned.1.call-done = bf16[1152,4608]{0,1:T(8,128)(2,1)} async-done(((bf16[1152,288]{0,1:T(8,128)(2,1)}), bf16[1152,4608]{0,1:T(8,128)(2,1)}) %all-gather.3.cloned.1.call-update) | async-done | bytes 10616848 | tf_op jit(solution)/shard_map/all_gather | solution.py:75
  137.5 11.9 %convolution_convert_fusion.1 = bf16[512,4608]{1,0:T(8,128)(2,1)} fusion(bf16[512,1152]{1,0:T(8,128)(2,1)S(1)} %copy-done, bf16[1152,4608]{0,1:T(8,128)(2,1)} %all-gather.3.cloned.1.call-done), kind=kOutput, calls=%fused_computation.2 | convolution fusion | flops 5438177280 | bytes 16515072 | tf_op jit(solution)/shard_map/dot_general | solution.py:73
  149.5 0.0 all-to-all-done.1
  149.5 5.3 %all-to-all-start = ((bf16[4,128,4608]{2,1,0:T(8,128)(2,1)}), bf16[4,128,4608]{2,1,0:T(8,128)(2,1)}, u32[]{:S(2)}, u32[]{:S(2)}) async-start(bf16[4,128,4608]{2,1,0:T(8,128)(2,1)} %bitcast.31), calls=%async_computation | async-start | bytes 9437184 | tf_op jit(solution)/shard_map/all_to_all | solution.py:28
  154.7 0.6 dynamic_slice.9
  155.3 0.6 iota_compare_fusion.1
  156.0 0.1 iota_compare_fusion
  156.1 92.9 %all-gather.5.cloned.1.call-done = bf16[64,16,4608]{2,1,0:T(8,128)(2,1)} async-done(((bf16[4,16,4608]{2,1,0:T(8,128)(2,1)}), bf16[64,16,4608]{2,1,0:T(8,128)(2,1)}) %all-gather.5.cloned.1.call-update) | async-done | bytes 9437200 | tf_op jit(solution)/shard_map/all_gather | solution.py:62
  249.0 12.8 %copy.10 = bf16[8,8,16,4608]{3,1,2,0:T(8,128)(2,1)} copy(bf16[8,8,16,4608]{3,2,1,0:T(8,128)(2,1)} %bitcast.29) | data formatting | bytes 18874368
  261.8 5.1 %fusion.7 = f32[1,73728]{1,0:T(1,128)S(1)} fusion(bf16[64,73728]{1,0:T(8,128)(2,1)} %bitcast.28, pred[4,64]{1,0:T(4,128)(4,1)S(1)} %iota_compare_fusion, s32[]{:T(128)S(6)} %select_n.9), kind=kOutput, calls=%fused_computation.13 | convolution fusion | flops 9437184 | bytes 9732356 | tf_op jit(solution)/shard_map/dot_general | solution.py:65
  266.9 0.2 reshape.51
  267.1 0.0 all-to-all-done
  267.1 3.3 %convert_reduce_fusion = f32[128,4608]{1,0:T(8,128)S(1)} fusion(bf16[4,128,4608]{2,1,0:T(8,128)(2,1)} %all-to-all-done), kind=kLoop, calls=%fused_computation.1 | loop fusion | flops 4128768 | bytes 7077888 | tf_op jit(solution)/shard_map/reduce_sum | solution.py:29
  270.4 1.5 fusion.2
  (7 shorter events, 0.0 us)
Async XLA Ops:
  6.5 4.2 %copy-start = (bf16[512,1152]{1,0:T(8,128)(2,1)S(1)}, bf16[512,1152]{1,0:T(8,128)(2,1)}, u32[]{:S(2)}) copy-start(bf16[512,1152]{1,0:T(8,128)(2,1)} %param.6) | copy-start | bytes 3538948
  6.5 131.0 %all-gather.3.cloned.1.call-start = ((), (), s32[]{:S(2)}) async-start(), calls=%async_computation.2 | async-start | bytes 11280384 | tf_op jit(solution)/shard_map/all_gather | solution.py:75
  7.3 241.8 %all-gather.5.cloned.1.call-start = ((), (), s32[]{:S(2)}) async-start(), calls=%async_computation.3 | async-start | bytes 10027008 | tf_op jit(solution)/shard_map/all_gather | solution.py:62
  8.0 2.2 copy-start.1
  11.8 137.6 %all-to-all-start.1 = ((f32[4,4,128,16]{2,3,1,0:T(8,128)}), f32[4,4,128,16]{2,3,1,0:T(8,128)S(1)}, u32[]{:S(2)}, u32[]{:S(2)}) async-start(f32[4,4,128,16]{2,3,1,0:T(8,128)} %broadcast_in_dim.11), calls=%async_computation.1 | async-start | bytes 262144 | tf_op jit(solution)/shard_map/all_to_all | solution.py:12
  149.5 5.3 %copy-start.2 = (s32[4]{0:T(128)S(1)}, s32[4]{0:T(128)}, u32[]{:S(2)}) copy-start(s32[4]{0:T(128)} %param.11) | copy-start | bytes 52
  149.5 117.6 %all-to-all-start = ((bf16[4,128,4608]{2,1,0:T(8,128)(2,1)}), bf16[4,128,4608]{2,1,0:T(8,128)(2,1)}, u32[]{:S(2)}, u32[]{:S(2)}) async-start(bf16[4,128,4608]{2,1,0:T(8,128)(2,1)} %bitcast.31), calls=%async_computation | async-start | bytes 9437184 | tf_op jit(solution)/shard_map/all_to_all | solution.py:28
Sparse Core Ops, SparseCore 0:
  9.1 128.3 all-gather.2
  139.3 109.6 all-gather.4
where the time goes:
time: 279 us
  waiting for transfers between devices  215 us (77%)
  matrix products  19.4 us (7%)
  local copies, waits for them, and re-layouts  16.5 us (6%)
  between operations  13.5 us (5%)
  starting transfers between devices  10.3 us (4%)
  other arithmetic  4.06 us (1%)
    all_gather x1, waiting for transfers between devices, body(): lax.all_gather(base_up_weight, 'gx', axis=1, tiled=True)  121 us
    all_gather x1, waiting for transfers between devices, body(): lax.all_gather(adapter_up_weight, 'gx', axis=0, tiled=True)  92.9 us
    unnamed x8, local copies, waits for them, and re-layouts  15 us
    dot_general x1, matrix products, body(): jnp.dot(tokens, lax.all_gather(base_up_weight, 'gx', axis=1, tiled=True),...  11.9 us
  transfers between devices with their start and end apart: 4, of which 2 were waited for; matrix products, arithmetic and copies ran while one was open for 13% of the time, Pallas kernels for 0%

commit v1 on v0

--- a/solution.py
+++ b/solution.py
@@ -1,10 +1,27 @@
+import functools
 import jax
 import jax.numpy as jnp
 from jax import lax
 from jax.sharding import PartitionSpec as P
+from jax.lax import all_to_all, axis_size
 
 ADAPTER_COUNT = 64
 BLOCK = 128
+
+
+def choose_spans(payload, dimension_no):
+    return jnp.concatenate(
+        all_to_all(
+            jnp.stack(tuple((payload for _ in range(axis_size("gx"))))),
+            axis_name="gx",
+            split_axis=0,
+            concat_axis=0,
+        ),
+        dimension_no,
+    )
+
+
+group_signs_in = functools.partial(choose_spans, dimension_no=1)
 
 
 def sent_to_all(array, axis):
@@ -71,9 +88,7 @@
     expand = jnp.einsum("bmr,brf->bmf", shrink_low, chosen_up, preferred_element_type=jnp.float32)
     expand = expand.reshape(own_rows, out_width)
     partial_value = jnp.dot(
-        tokens,
-        lax.all_gather(base_up_weight, "gx", axis=1, tiled=True),
-        preferred_element_type=jnp.float32,
+        tokens, group_signs_in(base_up_weight), preferred_element_type=jnp.float32
     )
     extra = 2.0 * expand
     total = summed_on_arrival(partial_value.astype(jnp.bfloat16), "gy", 0) + extra

time: 279 us -> 440 us (1.58)
  the two profiles are of different devices: /device:TPU:1 before, /device:TPU:166 now
where the time goes in v1:
time: 440 us
  waiting for transfers between devices  366 us (83%)
  local copies, waits for them, and re-layouts  20.6 us (5%)
  matrix products  19.3 us (4%)
  starting transfers between devices  16.1 us (4%)
  between operations  13.5 us (3%)
    all_to_all x1, waiting for transfers between devices, choose_spans(): all_to_all(jnp.stack(tuple((payload for _ in range(axis_size('gx'))))), a...  331 us
    all_to_all x1, waiting for transfers between devices, summed_on_arrival(): tiles = lax.all_to_all(in_blocks(array, dim, size), axis, 0, 0, tiled=True)  34.5 us
    unnamed x10, local copies, waits for them, and re-layouts  13.3 us
    dot_general x1, matrix products, body(): jnp.dot(tokens, group_signs_in(base_up_weight), preferred_element_type=jn...  11.9 us
  transfers between devices with their start and end apart: 4, of which 2 were waited for; matrix products, arithmetic and copies ran while one was open for 8% of the time, Pallas kernels for 0%

profile of v1, /device:TPU:166, one launch (start us, length us, event | category | flops | bytes accessed | tf_op | source)
XLA Modules:
  0.0 439.5 jit_solution(264797240698646366)
XLA Ops:
  6.5 5.8 %stack.2 = bf16[16,1152,288]{1,2,0:T(8,128)(2,1)} broadcast(bf16[1152,288]{0,1:T(8,128)(2,1)} %param.7), dimensions={1,2} | broadcast | bytes 11280384 | tf_op jit(solution)/shard_map/stack | solution.py:15
  12.4 6.7 %all-to-all-start = ((bf16[16,1152,288]{1,2,0:T(8,128)(2,1)}), bf16[16,1152,288]{1,2,0:T(8,128)(2,1)}, u32[]{:S(2)}, u32[]{:S(2)}) async-start(bf16[16,1152,288]{1,2,0:T(8,128)(2,1)} %stack.2), calls=%async_computation | async-start | bytes 21233664 | tf_op jit(solution)/shard_map/all_to_all | solution.py:14
  19.1 0.0 all-gather.2.cloned.1.call-start
  19.1 0.7 all-gather.2.cloned.1.call-update
  19.8 0.0 copy-start.2
  19.9 0.5 copy.10
  20.4 0.1 copy-done.2
  20.5 0.5 convolution_convert_fusion
  21.0 0.4 convolution_bitcast_fusion
  21.4 330.8 %all-to-all-done = bf16[16,1152,288]{1,2,0:T(8,128)(2,1)} async-done(((bf16[16,1152,288]{1,2,0:T(8,128)(2,1)}), bf16[16,1152,288]{1,2,0:T(8,128)(2,1)}, u32[]{:S(2)}, u32[]{:S(2)}) %all-to-all-start) | async-done | bytes 10616864 | tf_op jit(solution)/shard_map/all_to_all | solution.py:14
  352.2 0.7 broadcast_in_dim.11
  352.9 4.0 all-to-all-start.2
  356.9 11.9 %convolution_convert_fusion.1 = bf16[512,4608]{1,0:T(8,128)(2,1)} fusion(bf16[512,1152]{1,0:T(8,128)(2,1)S(1)} %copy-done, bf16[1152,4608]{0,1:T(8,128)(2,1)} %bitcast.2), kind=kOutput, calls=%fused_computation.2 | convolution fusion | flops 5438177280 | bytes 16515072 | tf_op jit(solution)/shard_map/dot_general | solution.py:90
  368.8 5.3 %all-to-all-start.1 = ((bf16[4,128,4608]{2,1,0:T(8,128)(2,1)}), bf16[4,128,4608]{2,1,0:T(8,128)(2,1)}, u32[]{:S(2)}, u32[]{:S(2)}) async-start(bf16[4,128,4608]{2,1,0:T(8,128)(2,1)} %bitcast.34), calls=%async_computation.1 | async-start | bytes 9437184 | tf_op jit(solution)/shard_map/all_to_all | solution.py:45
  374.1 0.6 dynamic_slice.9
  374.7 0.6 iota_compare_fusion.1
  375.4 0.1 iota_compare_fusion
  375.4 0.0 all-gather.2.cloned.1.call-done
  375.5 12.7 %copy.12 = bf16[8,8,16,4608]{3,1,2,0:T(8,128)(2,1)} copy(bf16[8,8,16,4608]{3,2,1,0:T(8,128)(2,1)} %bitcast.32) | data formatting | bytes 18874368
  388.2 5.0 %fusion.7 = f32[1,73728]{1,0:T(1,128)S(1)} fusion(bf16[64,73728]{1,0:T(8,128)(2,1)} %bitcast.31, pred[4,64]{1,0:T(4,128)(4,1)S(1)} %iota_compare_fusion, s32[]{:T(128)S(6)} %select_n.9), kind=kOutput, calls=%fused_computation.13 | convolution fusion | flops 9437184 | bytes 9732356 | tf_op jit(solution)/shard_map/dot_general | solution.py:82
  393.2 0.2 reshape.61
  393.4 34.5 %all-to-all-done.1 = bf16[4,128,4608]{2,1,0:T(8,128)(2,1)} async-done(((bf16[4,128,4608]{2,1,0:T(8,128)(2,1)}), bf16[4,128,4608]{2,1,0:T(8,128)(2,1)}, u32[]{:S(2)}, u32[]{:S(2)}) %all-to-all-start.1) | async-done | bytes 4718624 | tf_op jit(solution)/shard_map/all_to_all | solution.py:45
  427.9 3.3 convert_reduce_fusion
  431.2 1.5 fusion.2
  (9 shorter events, 0.0 us)
Async XLA Ops:
  6.5 14.4 %copy-start = (bf16[512,1152]{1,0:T(8,128)(2,1)S(1)}, bf16[512,1152]{1,0:T(8,128)(2,1)}, u32[]{:S(2)}) copy-start(bf16[512,1152]{1,0:T(8,128)(2,1)} %param.6) | copy-start | bytes 3538948
  12.4 7.5 %copy-start.1 = (bf16[64,16,1152]{2,1,0:T(8,128)(2,1)S(1)}, bf16[64,16,1152]{2,1,0:T(8,128)(2,1)}, u32[]{:S(2)}) copy-start(bf16[64,16,1152]{2,1,0:T(8,128)(2,1)} %param.8) | copy-start | bytes 7077892
  12.4 339.8 %all-to-all-start = ((bf16[16,1152,288]{1,2,0:T(8,128)(2,1)}), bf16[16,1152,288]{1,2,0:T(8,128)(2,1)}, u32[]{:S(2)}, u32[]{:S(2)}) async-start(bf16[16,1152,288]{1,2,0:T(8,128)(2,1)} %stack.2), calls=%async_computation | async-start | bytes 21233664 | tf_op jit(solution)/shard_map/all_to_all | solution.py:14
  19.1 356.4 %all-gather.2.cloned.1.call-start = ((), (), s32[]{:S(2)}) async-start(), calls=%async_computation.3 | async-start | bytes 10027008 | tf_op jit(solution)/shard_map/all_gather | solution.py:79
  19.8 0.7 copy-start.2
  352.9 15.9 %all-to-all-start.2 = ((f32[4,4,128,16]{2,3,1,0:T(8,128)}), f32[4,4,128,16]{2,3,1,0:T(8,128)S(1)}, u32[]{:S(2)}, u32[]{:S(2)}) async-start(f32[4,4,128,16]{2,3,1,0:T(8,128)} %broadcast_in_dim.11), calls=%async_computation.2 | async-start | bytes 262144 | tf_op jit(solution)/shard_map/all_to_all | solution.py:29
  368.8 5.3 %copy-start.3 = (s32[4]{0:T(128)S(1)}, s32[4]{0:T(128)}, u32[]{:S(2)}) copy-start(s32[4]{0:T(128)} %param.11) | copy-start | bytes 52
  368.8 59.1 %all-to-all-start.1 = ((bf16[4,128,4608]{2,1,0:T(8,128)(2,1)}), bf16[4,128,4608]{2,1,0:T(8,128)(2,1)}, u32[]{:S(2)}, u32[]{:S(2)}) async-start(bf16[4,128,4608]{2,1,0:T(8,128)(2,1)} %bitcast.34), calls=%async_computation.1 | async-start | bytes 9437184 | tf_op jit(solution)/shard_map/all_to_all | solution.py:45
Sparse Core Ops, SparseCore 0:
  21.7 323.3 all-gather.1
